TPU v7x, 32 devices: a whole 2x2x4 slice. The times are simulated.
32 devices in a mesh: grp: 2 (over y), bank: 4 (over z), seg: 4 (over x, core).
Axes of the slice: x: 2, y: 2, z: 4, core: 2. Of those that a mesh axis runs over, the one named last changes fastest.
Arguments:
- strain: bfloat16 [32, 2, 32768], P(('grp', 'seg'), None, 'bank'), parts along dimension 0, may hold values from -6 to 6
- templates: bfloat16 [4, 2, 32768], P('bank'), may hold values from -6 to 6
- length_bins: int32 [4], P('bank'), may hold values from 0 to 3
Outputs:
- snr_table: float32 [4, 32], P('bank', ('grp', 'seg')), parts along dimension 1
- segment_peak: float32 [32], P(('grp', 'seg')), parts along dimension 0
- template_peak: float32 [8], P(('grp', 'bank')), parts along dimension 0
There are 2 independent parts, one for each index of `grp`. A program takes and returns all parts, laid end to end along the dimension named above; an argument that names none is the same for every part. Nothing has to cross between parts.
All inputs are finite; a program needn't handle non-finite values.
Results may differ from a plain program's by a relative error of at most 0.0003.
Values may be sent and summed in bfloat16 or wider, within the bound.
A program may use at most 64 MiB of HBM per device.

v0:
```python
import math

import jax
import jax.numpy as jnp
from jax import lax
from jax.sharding import PartitionSpec as P

LEN = 32768
SQ_ROWS = 128
SQ_COLS = 256


EPSILON = 1e-06
HIGHEST = lax.Precision.HIGHEST


def shifted(block, axis, distance):
    devices = range(lax.axis_size(axis))
    route = [((i - distance) % len(devices), i) for i in devices]
    return lax.ppermute(block, axis, route)


def phase_pair(first, second, period):
    phases = (
        jnp.arange(first, dtype=jnp.int32)[:, None]
        * jnp.arange(second, dtype=jnp.int32)[None, :]
        % period
    )
    angles = phases.astype(jnp.float32) * (2.0 * math.pi / period)
    return (jnp.cos(angles), jnp.sin(angles))


def complex_einsum(form, left_real, left_imag, right_real, right_imag):
    out_real = jnp.einsum(form, left_real, right_real, precision=HIGHEST) - jnp.einsum(
        form, left_imag, right_imag, precision=HIGHEST
    )
    out_imag = jnp.einsum(form, left_real, right_imag, precision=HIGHEST) + jnp.einsum(
        form, left_imag, right_real, precision=HIGHEST
    )
    return (out_real, out_imag)


def square_power(prod_real, prod_imag, kept_rows, tables):
    row_real, row_imag, twist_real, twist_imag, col_real, col_imag = tables
    first_real, first_imag = complex_einsum("jk,bkc->bjc", row_real, row_imag, prod_real, prod_imag)
    turned_real = first_real * twist_real - first_imag * twist_imag
    turned_imag = first_real * twist_imag + first_imag * twist_real
    last_real, last_imag = complex_einsum(
        "bjc,ec->bje", turned_real, turned_imag, col_real, col_imag
    )
    return jnp.max(last_real * last_real + last_imag * last_imag, axis=(1, 2))


def template_peaks(prod_real, prod_imag, length_bins, power_fn, row_count, tables):
    seg_count = prod_real.shape[1]
    columns = LEN // row_count
    group = max(
        (divisor for divisor in range(1, min(seg_count, 8) + 1) if seg_count % divisor == 0)
    )
    shaped = (seg_count // group, group, row_count, columns)

    def one_template(inputs):
        many_real, many_imag, length_bin = inputs

        def one_group(pair):
            left_real, left_imag = pair
            return power_fn(left_real, left_imag, row_count, tables)

        powers = lax.map(one_group, (many_real.reshape(shaped), many_imag.reshape(shaped)))
        return powers.reshape(seg_count)

    return lax.map(one_template, (prod_real, prod_imag, length_bins))


def per_device(strain, templates, length_bins):
    row_count = SQ_ROWS
    row_real, row_imag = phase_pair(SQ_ROWS, SQ_ROWS, SQ_ROWS)
    twist_real, twist_imag = phase_pair(SQ_ROWS, SQ_COLS, LEN)
    col_real, col_imag = phase_pair(SQ_COLS, SQ_COLS, SQ_COLS)
    tables = (row_real, row_imag, twist_real, twist_imag, col_real, col_imag)
    tpl_count = templates.shape[0]
    seg_count = strain.shape[0]
    slab_width = strain.shape[2]
    bank_count = lax.axis_size("bank")
    own_index = lax.axis_index("bank")
    cutoffs = jnp.right_shift(jnp.int32(LEN), length_bins)
    tpl_real = templates[:, 0].astype(jnp.float32)
    tpl_imag = templates[:, 1].astype(jnp.float32)
    positions = jnp.arange(LEN, dtype=jnp.int32)
    keep_full = positions[None, :] < cutoffs[:, None]
    norm_real = jnp.where(keep_full, tpl_real, 0.0)
    norm_imag = jnp.where(keep_full, tpl_imag, 0.0)
    norm_values = jnp.sqrt(jnp.sum(norm_real * norm_real + norm_imag * norm_imag, axis=1) + EPSILON)

    def multiply(carry, piece, start):
        width = piece.shape[2]
        begin = jnp.asarray(start)
        part_real = lax.dynamic_slice_in_dim(tpl_real, begin, width, 1)
        part_imag = lax.dynamic_slice_in_dim(tpl_imag, begin, width, 1)
        keep_mask = (begin + jnp.arange(width, dtype=jnp.int32))[None, :] < cutoffs[:, None]
        part_real = jnp.where(keep_mask, part_real, 0.0)[:, None, :]
        part_imag = jnp.where(keep_mask, part_imag, 0.0)[:, None, :]
        seg_real = piece[:, 0].astype(jnp.float32)[None, :, :]
        seg_imag = piece[:, 1].astype(jnp.float32)[None, :, :]
        prod_real = part_real * seg_real + part_imag * seg_imag
        prod_imag = part_real * seg_imag - part_imag * seg_real
        anchor = (jnp.int32(0), jnp.int32(0), begin)
        return (
            lax.dynamic_update_slice(carry[0], prod_real, anchor),
            lax.dynamic_update_slice(carry[1], prod_imag, anchor),
        )

    empty = jnp.zeros((tpl_count, seg_count, LEN), jnp.float32)

    def advance(section_index, carry_state):
        strain_block, products = carry_state
        anchor = (own_index - section_index) % bank_count
        products = multiply(products, strain_block, anchor * slab_width)
        strain_block = shifted(strain_block, "bank", 1)
        return (strain_block, products)

    strain_block, products = lax.fori_loop(0, bank_count - 1, advance, (strain, (empty, empty)))
    anchor = (own_index - (bank_count - 1)) % bank_count
    prod_real, prod_imag = multiply(products, strain_block, anchor * slab_width)
    peak_power = template_peaks(prod_real, prod_imag, length_bins, square_power, row_count, tables)
    snr_table = jnp.sqrt(peak_power) / norm_values[:, None]
    segment_peak = lax.pmax(jnp.max(snr_table, axis=0), "bank")
    template_peak = lax.pmax(jnp.max(snr_table, axis=1), "seg")
    return (snr_table, segment_peak, template_peak)


def solution(mesh):
    placed = (P(("grp", "seg"), None, "bank"), P("bank", None, None), P("bank"))
    return jax.shard_map(
        per_device,
        mesh=mesh,
        in_specs=placed,
        out_specs=(P("bank", ("grp", "seg")), P(("grp", "seg")), P(("grp", "bank"))),
        check_vma=False,
    )
```

profile of v0, /device:TPU:0, one launch (start us, length us, event | category | flops | bytes accessed | tf_op | source)
XLA Modules:
  0.0 57.1 jit_solution(10657577971760804944)
XLA Ops:
  0.7 0.9 %copy-done.1 = bf16[1,2,32768]{2,1,0:T(2,128)(2,1)S(1)} copy-done((bf16[1,2,32768]{2,1,0:T(2,128)(2,1)S(1)}, bf16[1,2,32768]{2,1,0:T(2,128)(2,1)}, u32[]{:S(2)}) %copy-start.1) | copy-done | bytes 131096
  1.5 0.3 slice_convert_fusion.1
  2.7 0.8 %copy-done = bf16[4,2,8192]{2,1,0:T(2,128)(2,1)S(1)} copy-done((bf16[4,2,8192]{2,1,0:T(2,128)(2,1)S(1)}, bf16[4,2,8192]{2,1,0:T(2,128)(2,1)}, u32[]{:S(2)}) %copy-start) | copy-done | bytes 131096
  3.5 22.6 %while.18 = (s32[]{:T(128)}, bf16[4,2,8192]{2,1,0:T(2,128)(2,1)S(1)}, f32[1,4,32768]{2,1,0:T(4,128)S(1)}, f32[1,4,32768]{2,1,0:T(4,128)S(1)}, s32[]{:T(128)}, /*...) while((s32[]{:T(128)}, ...), condition=%wide.region_1.2_spmd, body=%wide.region_0.1_spmd.sunk | while | flops 311314 | bytes 1900912 | solution.py:122
  3.5 0.1 copy.60
  3.6 3.1 %collective-permute-start = (bf16[4,2,8192]{2,1,0:T(2,128)(2,1)S(1)}, bf16[4,2,8192]{2,1,0:T(2,128)(2,1)S(1)}, u32[]{:S(2)}, u32[]{:S(2)}) collective-permute-start(bf16[4,2,8192]{2,1,0:T(2,128)(2,1)S(1)} %copy.60), channel_id=1, source_target_pairs={{12,0},{0,4},{4,8},{8,12},{13,1},{1,5},{5,9},{9,13},{14,2},{2,6},{... | collective-permute-start | bytes 393224 | tf_op jit(solution)/shard_map/while/body/eval_jaxpr/ppermute | solution.py:20
  6.8 0.3 fusion.104
  7.1 0.2 copy_dynamic-update-slice_fusion.3
  7.3 4.9 %collective-permute-done = bf16[4,2,8192]{2,1,0:T(2,128)(2,1)S(1)} collective-permute-done((bf16[4,2,8192]{2,1,0:T(2,128)(2,1)S(1)}, bf16[4,2,8192]{2,1,0:T(2,128)(2,1)S(1)}, u32[]{:S(2)}, u32[]{:S(2)}) %collective-permute-start) | collective-permute-done | bytes 131104 | tf_op jit(solution)/shard_map/while/body/eval_jaxpr/ppermute | solution.py:20
  12.2 0.1 copy.60
  12.5 0.3 fusion.104
  12.9 0.2 copy_dynamic-update-slice_fusion.3
  13.1 6.1 %collective-permute-done = bf16[4,2,8192]{2,1,0:T(2,128)(2,1)S(1)} collective-permute-done((bf16[4,2,8192]{2,1,0:T(2,128)(2,1)S(1)}, bf16[4,2,8192]{2,1,0:T(2,128)(2,1)S(1)}, u32[]{:S(2)}, u32[]{:S(2)}) %collective-permute-start) | collective-permute-done | bytes 131104 | tf_op jit(solution)/shard_map/while/body/eval_jaxpr/ppermute | solution.py:20
  19.5 0.3 fusion.104
  19.8 0.2 copy_dynamic-update-slice_fusion.3
  20.0 6.1 %collective-permute-done = bf16[4,2,8192]{2,1,0:T(2,128)(2,1)S(1)} collective-permute-done((bf16[4,2,8192]{2,1,0:T(2,128)(2,1)S(1)}, bf16[4,2,8192]{2,1,0:T(2,128)(2,1)S(1)}, u32[]{:S(2)}, u32[]{:S(2)}) %collective-permute-start) | collective-permute-done | bytes 131104 | tf_op jit(solution)/shard_map/while/body/eval_jaxpr/ppermute | solution.py:20
  26.1 0.1 copy.6
  26.2 0.1 fusion.31
  26.3 1.2 %fusion.12 = f32[4,256,128]{2,1,0:T(8,128)S(1)} fusion(f32[1,4,128,256]{3,1,2,0:T(4,128)S(1)} %bitcast.89), kind=kOutput, calls=%fused_computation.25 | convolution fusion | flops 201555968 | bytes 1048576 | tf_op jit(solution)/shard_map/while/body/eval_jaxpr/while/body/eval_jaxpr/jk,bkc->bjc/dot_general | solution.py:34
  27.5 1.2 %fusion.3 = f32[4,128,256]{1,2,0:T(8,128)S(1)} fusion(f32[4,256,128]{2,1,0:T(8,128)S(1)} %fusion.12, f32[1,4,128,256]{3,1,2,0:T(4,128)S(1)} %bitcast.92), kind=kOutput, calls=%fused_computation.14 | convolution fusion | flops 201687040 | bytes 1572864 | tf_op jit(solution)/shard_map/while/body/eval_jaxpr/while/body/eval_jaxpr/jk,bkc->bjc/dot_general | solution.py:34
  28.7 1.2 %fusion.8 = f32[4,256,128]{2,1,0:T(8,128)S(1)} fusion(f32[1,4,128,256]{3,1,2,0:T(4,128)S(1)} %bitcast.93), kind=kOutput, calls=%fused_computation.21 | convolution fusion | flops 201555968 | bytes 1048576 | tf_op jit(solution)/shard_map/while/body/eval_jaxpr/while/body/eval_jaxpr/jk,bkc->bjc/dot_general | solution.py:37
  29.8 1.2 %fusion.2 = f32[4,128,256]{1,2,0:T(8,128)S(1)} fusion(f32[4,256,128]{2,1,0:T(8,128)S(1)} %fusion.8, f32[1,4,128,256]{3,1,2,0:T(4,128)S(1)} %bitcast.90), kind=kOutput, calls=%fused_computation.12 | convolution fusion | flops 201687040 | bytes 1572864 | tf_op jit(solution)/shard_map/while/body/eval_jaxpr/while/body/eval_jaxpr/jk,bkc->bjc/dot_general | solution.py:37
  31.0 0.5 fusion.57
  31.6 1.9 %fusion.21 = f32[4,128,256]{2,1,0:T(8,128)S(1)} fusion(f32[4,128,256]{1,2,0:T(8,128)S(1)} %fusion.2, f32[4,128,256]{1,2,0:T(8,128)S(1)} %fusion.3, f32[128,256]{0,1:T(8,128)S(1)} %get-tuple-element.307, f32[128,256]{0,1:T(8,128)S(1)} %get-tuple-element.308), kind=kOutput, calls=%fused_computation.41 | convolution fusion | flops 403963904 | bytes 1835008 | tf_op jit(solution)/shard_map/while/body/eval_jaxpr/while/body/eval_jaxpr/bjc,ec->bje/dot_general | solution.py:37
  33.4 1.9 %fusion.25 = f32[4,128,256]{2,1,0:T(8,128)S(1)} fusion(f32[4,128,256]{1,2,0:T(8,128)S(1)} %fusion.2, f32[4,128,256]{1,2,0:T(8,128)S(1)} %fusion.3, f32[128,256]{0,1:T(8,128)S(1)} %get-tuple-element.307, f32[128,256]{0,1:T(8,128)S(1)} %get-tuple-element.308), kind=kOutput, calls=%fused_computation.45 | convolution fusion | flops 403963904 | bytes 1835008 | tf_op jit(solution)/shard_map/while/body/eval_jaxpr/while/body/eval_jaxpr/bjc,ec->bje/dot_general | solution.py:34
  35.3 1.9 %fusion.6 = f32[4,128,256]{2,1,0:T(8,128)S(1)} fusion(f32[4,128,256]{2,1,0:T(8,128)S(1)} %fusion.25, f32[4,128,256]{1,2,0:T(8,128)S(1)} %fusion.2, f32[4,128,256]{1,2,0:T(8,128)S(1)} %fusion.3, f32[128,256]{0,1:T(8,128)S(1)} %get-tuple-element.307, f32[128,256]{0,1:T(8,128)S(1)} %get-tuple-element.308), kind=kOutput, calls=%fused_computation.19 | convolution fusion | flops 404226048 | bytes 2359296 | tf_op jit(solution)/shard_map/while/body/eval_jaxpr/while/body/eval_jaxpr/bjc,ec->bje/dot_general | solution.py:34
  37.2 2.0 %fusion.7 = f32[4]{0:T(128)S(1)} fusion(f32[4,128,256]{2,1,0:T(8,128)S(1)} %fusion.6, f32[4,128,256]{2,1,0:T(8,128)S(1)} %fusion.21, f32[4,128,256]{1,2,0:T(8,128)S(1)} %fusion.2, f32[4,128,256]{1,2,0:T(8,128)S(1)} %fusion.3, f32[128,256]{0,1:T(8,128)S(1)} %get-tuple-element.307, f32[128,256]{0,1:T(8,128)S(1)} %get-tuple-element.308), kind=kOutput, calls=%fused_computation.20 | convolution fusion | flops 404488192 | bytes 2359312 | tf_op jit(solution)/shard_map/while/body/eval_jaxpr/while/body/eval_jaxpr/bjc,ec->bje/dot_general | solution.py:37
  39.1 1.0 %fusion.49 = f32[]{:T(128)} fusion(s32[]{:T(128)} %bitcast.9, bf16[1,2,32768]{2,1,0:T(2,128)(2,1)S(1)} %copy-done.1), kind=kLoop, calls=%fused_computation.74 | loop fusion | flops 294911 | bytes 131080 | tf_op jit(solution)/shard_map/reduce_sum | solution.py:93
  40.8 0.6 %fusion.102 = (f32[]{:T(128)}, f32[4]{0:T(128)S(1)}) fusion(f32[]{:T(128)S(6)} %sqrt.19, f32[4]{0:T(128)S(1)} %fusion.7), kind=kLoop, calls=%fused_computation.132 | loop fusion | flops 7 | bytes 40 | tf_op jit(solution)/shard_map/reduce_max | solution.py:128
  41.5 0.5 copy-done.2
  42.0 8.8 %pmax.14 = f32[4]{0:T(128)} all-reduce(f32[4]{0:T(128)S(1)} %get-tuple-element.294), channel_id=1, replica_groups=mesh['grp'=2,'bank'=4,'seg'=4] {'bank'}, use_global_device_ids=true, to_apply=%region_4.5 | all-reduce | flops 4 | bytes 32 | tf_op jit(solution)/shard_map/pmax | solution.py:127
  50.8 6.3 %pmax.15 = f32[1]{0:T(128)} all-reduce(f32[1]{0:T(128)} %bitcast.25), channel_id=1, replica_groups=mesh['grp'=2,'bank'=4,'seg'=4] {'seg'}, use_global_device_ids=true, to_apply=%region_6.7 | all-reduce | flops 1 | bytes 8 | tf_op jit(solution)/shard_map/pmax | solution.py:128
  (15 shorter events, 0.7 us)
Async XLA Ops:
  0.6 0.9 %copy-start.1 = (bf16[1,2,32768]{2,1,0:T(2,128)(2,1)S(1)}, bf16[1,2,32768]{2,1,0:T(2,128)(2,1)}, u32[]{:S(2)}) copy-start(bf16[1,2,32768]{2,1,0:T(2,128)(2,1)} %param.6) | copy-start | bytes 393220
  2.6 0.9 %copy-start = (bf16[4,2,8192]{2,1,0:T(2,128)(2,1)S(1)}, bf16[4,2,8192]{2,1,0:T(2,128)(2,1)}, u32[]{:S(2)}) copy-start(bf16[4,2,8192]{2,1,0:T(2,128)(2,1)} %param.5) | copy-start | bytes 393220
  3.6 8.6 %collective-permute-start = (bf16[4,2,8192]{2,1,0:T(2,128)(2,1)S(1)}, bf16[4,2,8192]{2,1,0:T(2,128)(2,1)S(1)}, u32[]{:S(2)}, u32[]{:S(2)}) collective-permute-start(bf16[4,2,8192]{2,1,0:T(2,128)(2,1)S(1)} %copy.60), channel_id=1, source_target_pairs={{12,0},{0,4},{4,8},{8,12},{13,1},{1,5},{5,9},{9,13},{14,2},{2,6},{... | collective-permute-start | bytes 393224 | tf_op jit(solution)/shard_map/while/body/eval_jaxpr/ppermute | solution.py:20
  12.3 6.8 %collective-permute-start = (bf16[4,2,8192]{2,1,0:T(2,128)(2,1)S(1)}, bf16[4,2,8192]{2,1,0:T(2,128)(2,1)S(1)}, u32[]{:S(2)}, u32[]{:S(2)}) collective-permute-start(bf16[4,2,8192]{2,1,0:T(2,128)(2,1)S(1)} %copy.60), channel_id=1, source_target_pairs={{12,0},{0,4},{4,8},{8,12},{13,1},{1,5},{5,9},{9,13},{14,2},{2,6},{... | collective-permute-start | bytes 393224 | tf_op jit(solution)/shard_map/while/body/eval_jaxpr/ppermute | solution.py:20
  19.3 6.8 %collective-permute-start = (bf16[4,2,8192]{2,1,0:T(2,128)(2,1)S(1)}, bf16[4,2,8192]{2,1,0:T(2,128)(2,1)S(1)}, u32[]{:S(2)}, u32[]{:S(2)}) collective-permute-start(bf16[4,2,8192]{2,1,0:T(2,128)(2,1)S(1)} %copy.60), channel_id=1, source_target_pairs={{12,0},{0,4},{4,8},{8,12},{13,1},{1,5},{5,9},{9,13},{14,2},{2,6},{... | collective-permute-start | bytes 393224 | tf_op jit(solution)/shard_map/while/body/eval_jaxpr/ppermute | solution.py:20
  41.5 0.5 copy-start.2
where the time goes:
time: 57.3 us; the launch traced here: 57.1 us
  waiting for transfers between devices  17.1 us (30%)
  blocking collectives  15.1 us (26%)
  matrix products  12.3 us (21%)
  other arithmetic  3.79 us (7%)
  local copies, waits for them, and re-layouts  3.3 us (6%)
  starting transfers between devices  3.22 us (6%)
  between operations  2.1 us (4%)
    ppermute x3, waiting for transfers between devices, shifted(): return lax.ppermute(block, axis, route)  17.1 us
    pmax x1, blocking collectives, per_device(): segment_peak = lax.pmax(jnp.max(snr_table, axis=0), 'bank')  8.84 us
    pmax x1, blocking collectives, per_device(): template_peak = lax.pmax(jnp.max(snr_table, axis=1), 'seg')  6.27 us
    ppermute x3, starting transfers between devices, shifted(): return lax.ppermute(block, axis, route)  3.22 us
    dot_general x2, matrix products, complex_einsum(): jnp.einsum(form, left_imag, right_real, precision=HIGHEST)  3.14 us
    dot_general x2, matrix products, complex_einsum(): jnp.einsum(form, left_imag, right_imag, precision=HIGHEST)  3.05 us
    dot_general x2, matrix products, complex_einsum(): jnp.einsum(form, left_real, right_imag, precision=HIGHEST)  3.04 us
    dot_general x2, matrix products, complex_einsum(): jnp.einsum(form, left_real, right_real, precision=HIGHEST)  3.04 us
  transfers between devices with their start and end apart: 3, of which 3 were waited for; matrix products, arithmetic and copies ran while one was open for 3% of the time, Pallas kernels for 0%

commit v1 on v0

v1 whole, which is shorter than its diff:
```python
import functools
import math

import jax
import jax.numpy as jnp
import numpy as np
from jax import lax
from jax.experimental import pallas as pl
from jax.experimental.pallas import tpu as pltpu
from jax.sharding import PartitionSpec as P

MESH = pl.DeviceIdType.MESH
EPSILON = 1e-06
LANES = 128


def split(value):
    high = value.astype(jnp.bfloat16)
    low = (value - high.astype(jnp.float32)).astype(jnp.bfloat16)
    return high, low


def tables(length):
    rows = length // LANES
    half = rows // 2

    def root(phase, period):
        angle = 2.0 * math.pi * (phase % period) / period
        return np.cos(angle), np.sin(angle)

    r = np.arange(half)
    c = np.arange(LANES)
    row_c, row_s = root(np.outer(r, r), half)
    first = np.block([[row_c, -row_s], [row_s, row_c]])
    col_c, col_s = root(np.outer(c, c), LANES)
    last = np.block([[col_c, col_s], [-col_s, col_c]])
    odd = np.stack([np.broadcast_to(part[:, None], (half, LANES)) for part in root(r, rows)])
    turn = [root(np.outer(2 * r + p, c), length) for p in (0, 1)]
    turn = np.stack([np.concatenate([turn[0][i], turn[1][i]], axis=1) for i in (0, 1)])

    def halves(matrix):
        high = matrix.astype(jnp.bfloat16)
        low = (matrix - high.astype(np.float64)).astype(jnp.bfloat16)
        return high, low

    f_high, f_low = halves(first)
    l_high, l_low = halves(last)
    first = np.concatenate([f_high, f_high, f_low], axis=1)
    last = np.concatenate([l_high, l_high, l_low], axis=0)
    return first, last, odd.astype(np.float32), turn.astype(np.float32)


def kernel(
    banks, segs, chunks,
    strain_ref, tpl_ref, bins_ref, first_hbm, last_hbm, odd_hbm, turn_hbm,
    out_ref,
    held, tpl_re, tpl_im, work, first, last, odd, turn, row_bank, row_seg,
    table_sem, right_sem, left_sem, recv_sem, bank_send, bank_recv, seg_send, seg_recv,
):
    me = lax.axis_index("bank")
    my_seg = lax.axis_index("seg")
    count, depth, _ = strain_ref.shape
    size = count // chunks
    rows = tpl_ref.shape[0] // 2
    half = rows // 2

    barrier = pltpu.get_barrier_semaphore()
    has_left, has_right = me > 0, me < banks - 1

    @pl.when(has_left)
    def _():
        pl.semaphore_signal(barrier, inc=1, device_id={"bank": me - 1}, device_id_type=MESH)

    @pl.when(has_right)
    def _():
        pl.semaphore_signal(barrier, inc=1, device_id={"bank": me + 1}, device_id_type=MESH)

    for step in range(1, segs):
        pl.semaphore_signal(
            barrier, inc=1, device_id={"seg": lax.rem(my_seg + step, segs)}, device_id_type=MESH
        )
    loads = [
        pltpu.make_async_copy(source, target, table_sem.at[i])
        for i, (source, target) in enumerate(
            ((first_hbm, first), (odd_hbm, odd), (turn_hbm, turn), (last_hbm, last))
        )
    ]
    for load in loads:
        load.start()
    pl.semaphore_wait(barrier, has_left.astype(jnp.int32) + has_right.astype(jnp.int32) + segs - 1)

    def part(chunk):
        return pl.ds(chunk * size, size)

    def move(source, origin, chunk, step):
        sems = right_sem if step > 0 else left_sem
        return pltpu.make_async_remote_copy(
            src_ref=source,
            dst_ref=held.at[origin, part(chunk)],
            send_sem=sems.at[origin, chunk],
            recv_sem=recv_sem.at[origin, chunk],
            device_id={"bank": me + step},
            device_id_type=MESH,
        )

    for chunk in range(chunks):
        @pl.when(has_right)
        def _():
            move(strain_ref.at[part(chunk)], me, chunk, 1).start()

        @pl.when(has_left)
        def _():
            move(strain_ref.at[part(chunk)], me, chunk, -1).start()

    held[me] = strain_ref[...]

    work[...] = tpl_ref[...].astype(jnp.float32)
    position = lax.broadcasted_iota(jnp.int32, (rows, LANES), 0) * LANES
    position = position + lax.broadcasted_iota(jnp.int32, (rows, LANES), 1)
    keep = position < lax.shift_right_logical(jnp.int32(rows * LANES), bins_ref[0])
    real = jnp.where(keep, work[pl.ds(0, rows, stride=2), :], 0.0)
    imag = jnp.where(keep, work[pl.ds(1, rows, stride=2), :], 0.0)
    tpl_re[...] = real
    tpl_im[...] = imag
    sigma = jnp.sqrt(jnp.sum(real * real + imag * imag, keepdims=True) + EPSILON)

    for load in loads:
        load.wait()

    def peak(seg):
        work[...] = held[:, seg].reshape(2 * rows, LANES).astype(jnp.float32)
        s_re = work[pl.ds(0, rows, stride=2), :]
        s_im = work[pl.ds(1, rows, stride=2), :]
        h_re, h_im = tpl_re[...], tpl_im[...]
        q_re = h_re * s_re + h_im * s_im
        q_im = h_re * s_im - h_im * s_re
        even_re, even_im = q_re[:half] + q_re[half:], q_im[:half] + q_im[half:]
        d_re, d_im = q_re[:half] - q_re[half:], q_im[:half] - q_im[half:]
        odd_re = d_re * odd[0] - d_im * odd[1]
        odd_im = d_re * odd[1] + d_im * odd[0]
        y = jnp.concatenate(
            [
                jnp.concatenate([even_re, odd_re], axis=1),
                jnp.concatenate([even_im, odd_im], axis=1),
            ],
            axis=0,
        )
        high, low = split(y)
        u = jnp.dot(
            first[...],
            jnp.concatenate([high, low, high], axis=0),
            preferred_element_type=jnp.float32,
        )
        u_re, u_im = u[:half], u[half:]
        v_re = u_re * turn[0] - u_im * turn[1]
        v_im = u_re * turn[1] + u_im * turn[0]
        x = jnp.concatenate(
            [
                jnp.concatenate([v_re[:, :LANES], v_im[:, :LANES]], axis=1),
                jnp.concatenate([v_re[:, LANES:], v_im[:, LANES:]], axis=1),
            ],
            axis=0,
        )
        high, low = split(x)
        z = jnp.dot(
            jnp.concatenate([high, low, high], axis=1),
            last[...],
            preferred_element_type=jnp.float32,
        )
        z_re, z_im = z[:, :LANES], z[:, LANES:]
        power = z_re * z_re + z_im * z_im
        return jnp.max(power, keepdims=True)

    lane = lax.broadcasted_iota(jnp.int32, (8, LANES), 1)
    row = jnp.zeros((8, LANES), jnp.float32)
    for distance in range(1, banks):
        for chunk in range(chunks):
            for step in (1, -1):
                origin = me - step * distance
                inside = (origin >= 0) & (origin < banks)

                @pl.when(inside)
                def _():
                    block = held.at[origin, part(chunk)]
                    move(block, origin, chunk, step).wait_recv()

                    @pl.when((me + step >= 0) & (me + step < banks))
                    def _():
                        move(block, origin, chunk, step).start()

            if distance == banks - 1:
                for seg in range(chunk * size, (chunk + 1) * size):
                    row = jnp.where(lane == seg, jnp.sqrt(peak(seg)) / sigma, row)

    row_bank[me] = row
    row_seg[my_seg] = row

    def tell(buffer, axis, index, peer, send, recv):
        return pltpu.make_async_remote_copy(
            src_ref=buffer.at[index],
            dst_ref=buffer.at[index],
            send_sem=send.at[peer],
            recv_sem=recv.at[index],
            device_id={axis: peer},
            device_id_type=MESH,
        )

    groups = (
        (row_bank, "bank", me, banks, bank_send, bank_recv),
        (row_seg, "seg", my_seg, segs, seg_send, seg_recv),
    )
    for buffer, axis, index, number, send, recv in groups:
        for step in range(1, number):
            tell(buffer, axis, index, lax.rem(index + step, number), send, recv).start()
    for chunk in range(chunks):
        for step, sems in ((1, right_sem), (-1, left_sem)):
            for distance in range(banks):
                origin = me - step * distance

                @pl.when((origin >= 0) & (origin < banks) & (me + step >= 0) & (me + step < banks))
                def _():
                    move(held.at[origin, part(chunk)], origin, chunk, step).wait_send()

    for buffer, axis, index, number, send, recv in reversed(groups):
        for step in range(1, number):
            other = lax.rem(index + step, number)
            tell(buffer, axis, other, other, send, recv).wait_recv()
    segment_peak = jnp.max(row_bank[...], axis=0)
    template_peak = jnp.max(row_seg[...], keepdims=True)[0]
    line = lax.broadcasted_iota(jnp.int32, (8, LANES), 0)
    out_ref[...] = jnp.where(line == 0, row, jnp.where(line == 1, segment_peak, template_peak))
    for buffer, axis, index, number, send, recv in groups:
        for step in range(1, number):
            tell(buffer, axis, index, lax.rem(index + step, number), send, recv).wait_send()


def per_device(banks, segs, strain, templates, length_bins):
    count, _, width = strain.shape
    length = templates.shape[2]
    depth, rows = width // LANES, length // LANES
    chunks = count if banks <= 8 else 1
    first, last, odd, turn = tables(length)
    strain = strain.reshape(count, 2, depth, LANES).transpose(0, 2, 1, 3).reshape(count, 2 * depth, LANES)
    tpl = templates.reshape(2, rows, LANES).transpose(1, 0, 2).reshape(2 * rows, LANES)
    vmem = pl.BlockSpec(memory_space=pltpu.VMEM)
    smem = pl.BlockSpec(memory_space=pltpu.SMEM)
    hbm = pl.BlockSpec(memory_space=pl.ANY)
    dma = pltpu.SemaphoreType.DMA
    out = pl.pallas_call(
        functools.partial(kernel, banks, segs, chunks),
        out_shape=jax.ShapeDtypeStruct((8, LANES), jnp.float32),
        in_specs=[vmem, vmem, smem, hbm, hbm, hbm, hbm],
        out_specs=vmem,
        scratch_shapes=[
            pltpu.VMEM((banks, count, 2 * depth, LANES), jnp.bfloat16),
            pltpu.VMEM((rows, LANES), jnp.float32),
            pltpu.VMEM((rows, LANES), jnp.float32),
            pltpu.VMEM((2 * rows, LANES), jnp.float32),
            pltpu.VMEM(first.shape, first.dtype),
            pltpu.VMEM(last.shape, last.dtype),
            pltpu.VMEM(odd.shape, odd.dtype),
            pltpu.VMEM(turn.shape, turn.dtype),
            pltpu.VMEM((banks, 8, LANES), jnp.float32),
            pltpu.VMEM((segs, 8, LANES), jnp.float32),
            dma((4,)),
            dma((banks, chunks)),
            dma((banks, chunks)),
            dma((banks, chunks)),
            dma((banks,)),
            dma((banks,)),
            dma((segs,)),
            dma((segs,)),
        ],
        compiler_params=pltpu.CompilerParams(collective_id=0, has_side_effects=True),
        name="search",
    )(strain, tpl, length_bins, first, last, odd, turn)
    return out[0:1, :count], out[1, :count], out[2, 0:1]


def solution(mesh):
    placed = (P(("grp", "seg"), None, "bank"), P("bank", None, None), P("bank"))
    return jax.shard_map(
        functools.partial(per_device, mesh.shape["bank"], mesh.shape["seg"]),
        mesh=mesh,
        in_specs=placed,
        out_specs=(P("bank", ("grp", "seg")), P(("grp", "seg")), P(("grp", "bank"))),
        check_vma=False,
    )
```

time: 57.3 us -> 26.4 us (0.46)
  Pallas kernels: 0 us -> 22.4 us
  waiting for transfers between devices: 17.1 us -> 0 us
  blocking collectives: 15.1 us -> 0 us
  matrix products: 12.3 us -> 0 us
  other arithmetic: 3.79 us -> 0 us
  starting transfers between devices: 3.22 us -> 0 us
  local copies, waits for them, and re-layouts: 3.3 us -> 2.45 us
  between operations: 2.1 us -> 1.29 us
    pallas_call x0 -> x1, Pallas kernels: none -> 22.4 us  [per_device(): pl.pallas_call(functools.partial(kernel, banks, segs, chunks), out_shape=...]
    ppermute x3 -> x0, waiting for transfers between devices: 17.1 us -> none  [shifted(): return lax.ppermute(block, axis, route)]
    pmax x2 -> x0, blocking collectives: 15.1 us -> none  [the longest x1 8.84 us: per_device(): segment_peak = lax.pmax(jnp.max(snr_table, axis=0), 'bank')]
    dot_general x8 -> x0, matrix products: 12.3 us -> none  [the longest x2 3.14 us: complex_einsum(): jnp.einsum(form, left_imag, right_real, precision=HIGHEST)]
    ppermute x3 -> x0, starting transfers between devices: 3.22 us -> none  [shifted(): return lax.ppermute(block, axis, route)]
    unnamed x6 -> x0, local copies, waits for them, and re-layouts: 2.2 us -> none
    squeeze x0 -> x1, local copies, waits for them, and re-layouts: none -> 1.26 us  [per_device(): return (out[0:1, :count], out[1, :count], out[2, 0:1])]
    slice x0 -> x1, local copies, waits for them, and re-layouts: none -> 1.18 us  [per_device(): return (out[0:1, :count], out[1, :count], out[2, 0:1])]
  transfers between devices with their start and end apart: 3 -> 0, of which waited for: 3 -> 0; matrix products, arithmetic and copies ran while one was open for 3% -> 0% of each run, Pallas kernels for 0% -> 0%
where the time goes in v1:
time: 26.4 us; the launch traced here: 26.2 us
  Pallas kernels  22.4 us (85%)
  local copies, waits for them, and re-layouts  2.45 us (9%)
  between operations  1.29 us (5%)
    pallas_call x1, Pallas kernels, per_device(): pl.pallas_call(functools.partial(kernel, banks, segs, chunks), out_shape=...  22.4 us
    squeeze x1, local copies, waits for them, and re-layouts, per_device(): return (out[0:1, :count], out[1, :count], out[2, 0:1])  1.26 us
    slice x1, local copies, waits for them, and re-layouts, per_device(): return (out[0:1, :count], out[1, :count], out[2, 0:1])  1.18 us

profile of v1, /device:TPU:0, one launch (start us, length us, event | category | flops | bytes accessed | tf_op | source)
XLA Modules:
  0.0 26.2 jit_solution(10467070183078113194)
XLA Ops:
  1.3 22.4 %search.1 = f32[8,128]{1,0:T(8,128)} custom-call(bf16[4,128,128]{2,1,0:T(8,128)(2,1)} %bitcast.13, bf16[512,128]{1,0:T(8,128)(2,1)} %bitcast.14, s32[1]{0:T(128)S(6)} %copy.12.bins_ref, bf16[256,768]{1,0:T(8,128)(2,1)} %constant.8.clone.first_hbm, bf16[768,256]{1,0:T(8,128)(2,1)} %constant.9.clone.last_hbm, f32[2,128,128]{2,1,0:T(8,128)} %constant.10.clone.odd_hbm, ...), custom_call_target="tpu_custom_call" | custom-call | tf_op jit(solution)/shard_map/search/pallas_call | solution.py:249
  23.7 1.3 %slice_bitcast_fusion = (f32[4]{0:T(128)}, f32[1,4]{1,0:T(1,128)}) fusion(f32[8,128]{1,0:T(8,128)} %search.1), kind=kLoop, calls=%fused_computation | loop fusion | bytes 64 | tf_op jit(solution)/shard_map/squeeze | solution.py:277
  25.0 1.2 %slice.11 = f32[1,1]{1,0:T(1,128)} slice(f32[8,128]{1,0:T(8,128)} %search.1), slice={[2:3], [0:1]} | slice | bytes 8 | tf_op jit(solution)/shard_map/slice | solution.py:277

commit v2 on v1

--- a/solution.py
+++ b/solution.py
@@ -52,10 +52,10 @@
 
 def kernel(
     banks, segs, chunks,
-    strain_ref, tpl_ref, bins_ref, first_hbm, last_hbm, odd_hbm, turn_hbm,
+    strain_hbm, tpl_hbm, bins_ref, first_hbm, last_hbm, odd_hbm, turn_hbm,
     out_ref,
-    held, tpl_re, tpl_im, work, first, last, odd, turn, row_bank, row_seg,
-    table_sem, right_sem, left_sem, recv_sem, bank_send, bank_recv, seg_send, seg_recv,
+    strain_ref, tpl_ref, held, tpl_re, tpl_im, work, first, last, odd, turn, row_bank, row_seg,
+    input_sem, table_sem, right_sem, left_sem, recv_sem, bank_send, bank_recv, seg_send, seg_recv,
 ):
     me = lax.axis_index("bank")
     my_seg = lax.axis_index("seg")
@@ -64,6 +64,9 @@
     rows = tpl_ref.shape[0] // 2
     half = rows // 2
 
+    def part(chunk):
+        return pl.ds(chunk * size, size)
+
     barrier = pltpu.get_barrier_semaphore()
     has_left, has_right = me > 0, me < banks - 1
 
@@ -79,6 +82,15 @@
         pl.semaphore_signal(
             barrier, inc=1, device_id={"seg": lax.rem(my_seg + step, segs)}, device_id_type=MESH
         )
+    inputs = [
+        pltpu.make_async_copy(source, target, input_sem.at[i])
+        for i, (source, target) in enumerate(
+            [(strain_hbm.at[part(chunk)], strain_ref.at[part(chunk)]) for chunk in range(chunks)]
+            + [(tpl_hbm, tpl_ref)]
+        )
+    ]
+    for load in inputs:
+        load.start()
     loads = [
         pltpu.make_async_copy(source, target, table_sem.at[i])
         for i, (source, target) in enumerate(
@@ -88,9 +100,6 @@
     for load in loads:
         load.start()
     pl.semaphore_wait(barrier, has_left.astype(jnp.int32) + has_right.astype(jnp.int32) + segs - 1)
-
-    def part(chunk):
-        return pl.ds(chunk * size, size)
 
     def move(source, origin, chunk, step):
         sems = right_sem if step > 0 else left_sem
@@ -104,6 +113,8 @@
         )
 
     for chunk in range(chunks):
+        inputs[chunk].wait()
+
         @pl.when(has_right)
         def _():
             move(strain_ref.at[part(chunk)], me, chunk, 1).start()
@@ -114,10 +125,12 @@
 
     held[me] = strain_ref[...]
 
+    for load in inputs[chunks:]:
+        load.wait()
     work[...] = tpl_ref[...].astype(jnp.float32)
     position = lax.broadcasted_iota(jnp.int32, (rows, LANES), 0) * LANES
     position = position + lax.broadcasted_iota(jnp.int32, (rows, LANES), 1)
-    keep = position < lax.shift_right_logical(jnp.int32(rows * LANES), bins_ref[0])
+    keep = position < lax.shift_right_logical(jnp.full((1, 1), rows * LANES, jnp.int32), bins_ref[...])
     real = jnp.where(keep, work[pl.ds(0, rows, stride=2), :], 0.0)
     imag = jnp.where(keep, work[pl.ds(1, rows, stride=2), :], 0.0)
     tpl_re[...] = real
@@ -234,6 +247,12 @@
             tell(buffer, axis, index, lax.rem(index + step, number), send, recv).wait_send()
 
 
+def unpack(out_ref, table_ref, segment_ref, template_ref):
+    table_ref[...] = out_ref[0:1, : table_ref.shape[1]]
+    segment_ref[...] = out_ref[1, : segment_ref.shape[0]]
+    template_ref[...] = out_ref[2, :1]
+
+
 def per_device(banks, segs, strain, templates, length_bins):
     count, _, width = strain.shape
     length = templates.shape[2]
@@ -243,15 +262,16 @@
     strain = strain.reshape(count, 2, depth, LANES).transpose(0, 2, 1, 3).reshape(count, 2 * depth, LANES)
     tpl = templates.reshape(2, rows, LANES).transpose(1, 0, 2).reshape(2 * rows, LANES)
     vmem = pl.BlockSpec(memory_space=pltpu.VMEM)
-    smem = pl.BlockSpec(memory_space=pltpu.SMEM)
-    hbm = pl.BlockSpec(memory_space=pl.ANY)
+    hbm = pl.BlockSpec(memory_space=pltpu.HBM)
     dma = pltpu.SemaphoreType.DMA
     out = pl.pallas_call(
         functools.partial(kernel, banks, segs, chunks),
         out_shape=jax.ShapeDtypeStruct((8, LANES), jnp.float32),
-        in_specs=[vmem, vmem, smem, hbm, hbm, hbm, hbm],
+        in_specs=[hbm, hbm, vmem, hbm, hbm, hbm, hbm],
         out_specs=vmem,
         scratch_shapes=[
+            pltpu.VMEM(strain.shape, strain.dtype),
+            pltpu.VMEM(tpl.shape, tpl.dtype),
             pltpu.VMEM((banks, count, 2 * depth, LANES), jnp.bfloat16),
             pltpu.VMEM((rows, LANES), jnp.float32),
             pltpu.VMEM((rows, LANES), jnp.float32),
@@ -262,6 +282,7 @@
             pltpu.VMEM(turn.shape, turn.dtype),
             pltpu.VMEM((banks, 8, LANES), jnp.float32),
             pltpu.VMEM((segs, 8, LANES), jnp.float32),
+            dma((chunks + 1,)),
             dma((4,)),
             dma((banks, chunks)),
             dma((banks, chunks)),
@@ -273,8 +294,18 @@
         ],
         compiler_params=pltpu.CompilerParams(collective_id=0, has_side_effects=True),
         name="search",
-    )(strain, tpl, length_bins, first, last, odd, turn)
-    return out[0:1, :count], out[1, :count], out[2, 0:1]
+    )(strain, tpl, length_bins.reshape(1, 1), first, last, odd, turn)
+    return pl.pallas_call(
+        unpack,
+        out_shape=[
+            jax.ShapeDtypeStruct((1, count), jnp.float32),
+            jax.ShapeDtypeStruct((count,), jnp.float32),
+            jax.ShapeDtypeStruct((1,), jnp.float32),
+        ],
+        in_specs=[vmem],
+        out_specs=[vmem] * 3,
+        name="unpack",
+    )(out)
 
 
 def solution(mesh):

time: 26.4 us -> 24.3 us (0.920)
  local copies, waits for them, and re-layouts: 2.45 us -> 0 us
  Pallas kernels: 22.4 us -> 22.8 us
    squeeze x1 -> x0, local copies, waits for them, and re-layouts: 1.26 us -> none  [per_device(): return (out[0:1, :count], out[1, :count], out[2, 0:1])]
    pallas_call x0 -> x1, Pallas kernels: none -> 1.2 us  [per_device(): pl.pallas_call(unpack, out_shape=[jax.ShapeDtypeStruct((1, count), jnp.fl...]
    slice x1 -> x0, local copies, waits for them, and re-layouts: 1.18 us -> none  [per_device(): return (out[0:1, :count], out[1, :count], out[2, 0:1])]
    pallas_call x1, Pallas kernels: 22.4 us -> 21.6 us  [per_device(): pl.pallas_call(functools.partial(kernel, banks, segs, chunks), out_shape=...]
where the time goes in v2:
time: 24.3 us; the launch traced here: 24.1 us
  Pallas kernels  22.8 us (94%)
  between operations  1.28 us (5%)
    pallas_call x1, Pallas kernels, per_device(): pl.pallas_call(functools.partial(kernel, banks, segs, chunks), out_shape=...  21.6 us
    pallas_call x1, Pallas kernels, per_device(): pl.pallas_call(unpack, out_shape=[jax.ShapeDtypeStruct((1, count), jnp.fl...  1.2 us

profile of v2, /device:TPU:0, one launch (start us, length us, event | category | flops | bytes accessed | tf_op | source)
XLA Modules:
  0.0 24.1 jit_solution(1143783548833053159)
XLA Ops:
  1.3 21.6 %search.1.out_ref = f32[8,128]{1,0:T(8,128)} custom-call(bf16[4,128,128]{2,1,0:T(8,128)(2,1)} %bitcast.12, bf16[512,128]{1,0:T(8,128)(2,1)} %bitcast.13, s32[1,1]{1,0:T(1,128)} %bitcast.11.bins_ref, bf16[256,768]{1,0:T(8,128)(2,1)} %constant.8.clone.first_hbm, bf16[768,256]{1,0:T(8,128)(2,1)} %constant.9.clone.last_hbm, ...), custom_call_target="tpu_custom_call" | custom-call | tf_op jit(solution)/shard_map/search/pallas_call | solution.py:267
  22.9 1.2 %unpack.1 = (f32[1,4]{1,0:T(1,128)}, f32[4]{0:T(128)}, f32[1]{0:T(128)}) custom-call(f32[8,128]{1,0:T(8,128)} %search.1.out_ref), custom_call_target="tpu_custom_call" | custom-call | tf_op jit(solution)/shard_map/unpack/pallas_call | solution.py:298

commit v3 on v2

--- a/solution.py
+++ b/solution.py
@@ -51,11 +51,13 @@
 
 
 def kernel(
-    banks, segs, chunks,
+    banks, segs, chunks, give,
     strain_hbm, tpl_hbm, bins_ref, first_hbm, last_hbm, odd_hbm, turn_hbm,
     out_ref,
-    strain_ref, tpl_ref, held, tpl_re, tpl_im, work, first, last, odd, turn, row_bank, row_seg,
+    strain_ref, tpl_ref, masked, lent, held, tpl_re, tpl_im, two_re, two_im, work, first, last, odd, turn,
+    row_bank, row_seg, row_far,
     input_sem, table_sem, right_sem, left_sem, recv_sem, bank_send, bank_recv, seg_send, seg_recv,
+    far_send, far_recv, tpl_send, tpl_recv,
 ):
     me = lax.axis_index("bank")
     my_seg = lax.axis_index("seg")
@@ -69,6 +71,15 @@
 
     barrier = pltpu.get_barrier_semaphore()
     has_left, has_right = me > 0, me < banks - 1
+    is_end = jnp.logical_not(has_left & has_right) & (give > 0)
+    helps = ((me == 1) | (me == banks - 2)) & (give > 0)
+    helper = jnp.where(me == 0, 1, banks - 2)
+    helped = jnp.where(me == 1, 0, banks - 1)
+
+    def wanted(device, chunk):
+        least = 1 if chunk >= chunks - give else 0
+        return (device >= least) & (device < banks - least)
+
 
     @pl.when(has_left)
     def _():
@@ -82,6 +93,15 @@
         pl.semaphore_signal(
             barrier, inc=1, device_id={"seg": lax.rem(my_seg + step, segs)}, device_id_type=MESH
         )
+    if give:
+        for step in range(1, segs):
+            @pl.when(is_end)
+            def _():
+                pl.semaphore_signal(
+                    barrier, inc=1, device_id={"bank": helper, "seg": lax.rem(my_seg + step, segs)},
+                    device_id_type=MESH,
+                )
+
     inputs = [
         pltpu.make_async_copy(source, target, input_sem.at[i])
         for i, (source, target) in enumerate(
@@ -99,7 +119,7 @@
     ]
     for load in loads:
         load.start()
-    pl.semaphore_wait(barrier, has_left.astype(jnp.int32) + has_right.astype(jnp.int32) + segs - 1)
+    pl.semaphore_wait(barrier, has_left.astype(jnp.int32) + has_right.astype(jnp.int32) + segs - 1 + helps.astype(jnp.int32) * (segs - 1))
 
     def move(source, origin, chunk, step):
         sems = right_sem if step > 0 else left_sem
@@ -115,11 +135,11 @@
     for chunk in range(chunks):
         inputs[chunk].wait()
 
-        @pl.when(has_right)
+        @pl.when(wanted(me + 1, chunk))
         def _():
             move(strain_ref.at[part(chunk)], me, chunk, 1).start()
 
-        @pl.when(has_left)
+        @pl.when(wanted(me - 1, chunk))
         def _():
             move(strain_ref.at[part(chunk)], me, chunk, -1).start()
 
@@ -127,24 +147,40 @@
 
     for load in inputs[chunks:]:
         load.wait()
-    work[...] = tpl_ref[...].astype(jnp.float32)
-    position = lax.broadcasted_iota(jnp.int32, (rows, LANES), 0) * LANES
-    position = position + lax.broadcasted_iota(jnp.int32, (rows, LANES), 1)
+    position = lax.broadcasted_iota(jnp.int32, (2 * rows, LANES), 0) // 2 * LANES
+    position = position + lax.broadcasted_iota(jnp.int32, (2 * rows, LANES), 1)
     keep = position < lax.shift_right_logical(jnp.full((1, 1), rows * LANES, jnp.int32), bins_ref[...])
-    real = jnp.where(keep, work[pl.ds(0, rows, stride=2), :], 0.0)
-    imag = jnp.where(keep, work[pl.ds(1, rows, stride=2), :], 0.0)
-    tpl_re[...] = real
-    tpl_im[...] = imag
-    sigma = jnp.sqrt(jnp.sum(real * real + imag * imag, keepdims=True) + EPSILON)
+    value = jnp.where(keep, tpl_ref[...].astype(jnp.float32), 0.0)
+    if give:
+        masked[...] = value.astype(jnp.bfloat16)
+
+    def prepare(interleaved, re_ref, im_ref):
+        work[...] = interleaved
+        re_ref[...] = work[pl.ds(0, rows, stride=2), :]
+        im_ref[...] = work[pl.ds(1, rows, stride=2), :]
+        return jnp.sqrt(jnp.sum(interleaved * interleaved, keepdims=True) + EPSILON)
+
+    sigma = prepare(value, tpl_re, tpl_im)
+
+    def lend():
+        return pltpu.make_async_remote_copy(
+            src_ref=masked, dst_ref=lent, send_sem=tpl_send.at[0], recv_sem=tpl_recv.at[0],
+            device_id={"bank": helper}, device_id_type=MESH,
+        )
+
+    if give:
+        @pl.when(is_end)
+        def _():
+            lend().start()
 
     for load in loads:
         load.wait()
 
-    def peak(seg):
+    def peak(seg, re_ref, im_ref):
         work[...] = held[:, seg].reshape(2 * rows, LANES).astype(jnp.float32)
         s_re = work[pl.ds(0, rows, stride=2), :]
         s_im = work[pl.ds(1, rows, stride=2), :]
-        h_re, h_im = tpl_re[...], tpl_im[...]
+        h_re, h_im = re_ref[...], im_ref[...]
         q_re = h_re * s_re + h_im * s_im
         q_im = h_re * s_im - h_im * s_re
         even_re, even_im = q_re[:half] + q_re[half:], q_im[:half] + q_im[half:]
@@ -185,28 +221,44 @@
         return jnp.max(power, keepdims=True)
 
     lane = lax.broadcasted_iota(jnp.int32, (8, LANES), 1)
-    row = jnp.zeros((8, LANES), jnp.float32)
+    line = lax.broadcasted_iota(jnp.int32, (8, LANES), 0)
+    row_bank[me] = jnp.zeros((8, LANES), jnp.float32)
+
+    def note(seg, which, snr):
+        row_bank[me] = jnp.where((lane == seg) & (line == which), snr, row_bank[me])
+
     for distance in range(1, banks):
         for chunk in range(chunks):
             for step in (1, -1):
                 origin = me - step * distance
-                inside = (origin >= 0) & (origin < banks)
+                inside = (origin >= 0) & (origin < banks) & wanted(me, chunk)
 
                 @pl.when(inside)
                 def _():
                     block = held.at[origin, part(chunk)]
                     move(block, origin, chunk, step).wait_recv()
 
-                    @pl.when((me + step >= 0) & (me + step < banks))
+                    @pl.when(wanted(me + step, chunk))
                     def _():
                         move(block, origin, chunk, step).start()
 
             if distance == banks - 1:
                 for seg in range(chunk * size, (chunk + 1) * size):
-                    row = jnp.where(lane == seg, jnp.sqrt(peak(seg)) / sigma, row)
-
-    row_bank[me] = row
-    row_seg[my_seg] = row
+                    if chunk < chunks - give:
+                        note(seg, 0, jnp.sqrt(peak(seg, tpl_re, tpl_im)) / sigma)
+                        continue
+
+                    @pl.when(helps)
+                    def _():
+                        if chunk == chunks - give:
+                            lend().wait_recv()
+                        sigma_two = prepare(lent[...].astype(jnp.float32), two_re, two_im)
+                        one = peak(seg, tpl_re, tpl_im)
+                        two = peak(seg, two_re, two_im)
+                        note(seg, 0, jnp.sqrt(one) / sigma)
+                        note(seg, 1, jnp.sqrt(two) / sigma_two)
+
+    row_seg[my_seg] = row_bank[me]
 
     def tell(buffer, axis, index, peer, send, recv):
         return pltpu.make_async_remote_copy(
@@ -218,6 +270,20 @@
             device_id_type=MESH,
         )
 
+    def far(peer):
+        return pltpu.make_async_remote_copy(
+            src_ref=row_seg.at[my_seg], dst_ref=row_far.at[my_seg],
+            send_sem=far_send.at[peer], recv_sem=far_recv.at[my_seg],
+            device_id={"bank": helped, "seg": peer}, device_id_type=MESH,
+        )
+
+    def heard(peer):
+        return pltpu.make_async_remote_copy(
+            src_ref=row_seg.at[my_seg], dst_ref=row_far.at[peer],
+            send_sem=far_send.at[peer], recv_sem=far_recv.at[peer],
+            device_id={"bank": helper, "seg": peer}, device_id_type=MESH,
+        )
+
     groups = (
         (row_bank, "bank", me, banks, bank_send, bank_recv),
         (row_seg, "seg", my_seg, segs, seg_send, seg_recv),
@@ -225,12 +291,18 @@
     for buffer, axis, index, number, send, recv in groups:
         for step in range(1, number):
             tell(buffer, axis, index, lax.rem(index + step, number), send, recv).start()
+    peers = [lax.rem(my_seg + step, segs) for step in range(1, segs)]
+    if give:
+        @pl.when(helps)
+        def _():
+            for peer in peers:
+                far(peer).start()
     for chunk in range(chunks):
         for step, sems in ((1, right_sem), (-1, left_sem)):
             for distance in range(banks):
                 origin = me - step * distance
 
-                @pl.when((origin >= 0) & (origin < banks) & (me + step >= 0) & (me + step < banks))
+                @pl.when((origin >= 0) & (origin < banks) & wanted(me + step, chunk))
                 def _():
                     move(held.at[origin, part(chunk)], origin, chunk, step).wait_send()
 
@@ -238,10 +310,38 @@
         for step in range(1, number):
             other = lax.rem(index + step, number)
             tell(buffer, axis, other, other, send, recv).wait_recv()
-    segment_peak = jnp.max(row_bank[...], axis=0)
-    template_peak = jnp.max(row_seg[...], keepdims=True)[0]
-    line = lax.broadcasted_iota(jnp.int32, (8, LANES), 0)
-    out_ref[...] = jnp.where(line == 0, row, jnp.where(line == 1, segment_peak, template_peak))
+    segment_peak = jnp.max(row_bank[...], axis=(0, 1))[None, :]
+    table = row_bank[me][:1]
+    template_row = jnp.max(row_seg[...], axis=0)[:1]
+
+    def give_out(table, template_row):
+        template_peak = jnp.max(template_row, axis=1, keepdims=True)
+        out_ref[...] = jnp.where(line == 0, table, jnp.where(line == 1, segment_peak, template_peak))
+
+    if give:
+        @pl.when(is_end)
+        def _():
+            theirs = row_bank[helper][1:2]
+            every = jnp.maximum(template_row, theirs)
+            for peer in peers:
+                heard(peer).wait_recv()
+                every = jnp.maximum(every, row_far[peer][1:2])
+            give_out(jnp.maximum(table, theirs), every)
+
+        @pl.when(jnp.logical_not(is_end))
+        def _():
+            give_out(table, template_row)
+
+        @pl.when(is_end)
+        def _():
+            lend().wait_send()
+
+        @pl.when(helps)
+        def _():
+            for peer in peers:
+                far(peer).wait_send()
+    else:
+        give_out(table, template_row)
     for buffer, axis, index, number, send, recv in groups:
         for step in range(1, number):
             tell(buffer, axis, index, lax.rem(index + step, number), send, recv).wait_send()
@@ -258,6 +358,7 @@
     length = templates.shape[2]
     depth, rows = width // LANES, length // LANES
     chunks = count if banks <= 8 else 1
+    give = 1 if banks == 4 and chunks == count > 1 else 0
     first, last, odd, turn = tables(length)
     strain = strain.reshape(count, 2, depth, LANES).transpose(0, 2, 1, 3).reshape(count, 2 * depth, LANES)
     tpl = templates.reshape(2, rows, LANES).transpose(1, 0, 2).reshape(2 * rows, LANES)
@@ -265,14 +366,18 @@
     hbm = pl.BlockSpec(memory_space=pltpu.HBM)
     dma = pltpu.SemaphoreType.DMA
     out = pl.pallas_call(
-        functools.partial(kernel, banks, segs, chunks),
+        functools.partial(kernel, banks, segs, chunks, give),
         out_shape=jax.ShapeDtypeStruct((8, LANES), jnp.float32),
         in_specs=[hbm, hbm, vmem, hbm, hbm, hbm, hbm],
         out_specs=vmem,
         scratch_shapes=[
             pltpu.VMEM(strain.shape, strain.dtype),
             pltpu.VMEM(tpl.shape, tpl.dtype),
+            pltpu.VMEM(tpl.shape, tpl.dtype),
+            pltpu.VMEM(tpl.shape, tpl.dtype),
             pltpu.VMEM((banks, count, 2 * depth, LANES), jnp.bfloat16),
+            pltpu.VMEM((rows, LANES), jnp.float32),
+            pltpu.VMEM((rows, LANES), jnp.float32),
             pltpu.VMEM((rows, LANES), jnp.float32),
             pltpu.VMEM((rows, LANES), jnp.float32),
             pltpu.VMEM((2 * rows, LANES), jnp.float32),
@@ -281,6 +386,7 @@
             pltpu.VMEM(odd.shape, odd.dtype),
             pltpu.VMEM(turn.shape, turn.dtype),
             pltpu.VMEM((banks, 8, LANES), jnp.float32),
+            pltpu.VMEM((segs, 8, LANES), jnp.float32),
             pltpu.VMEM((segs, 8, LANES), jnp.float32),
             dma((chunks + 1,)),
             dma((4,)),
@@ -291,6 +397,10 @@
             dma((banks,)),
             dma((segs,)),
             dma((segs,)),
+            dma((segs,)),
+            dma((segs,)),
+            dma((1,)),
+            dma((1,)),
         ],
         compiler_params=pltpu.CompilerParams(collective_id=0, has_side_effects=True),
         name="search",

time: 24.3 us -> 23.7 us (0.975)
  Pallas kernels: 22.8 us -> 22.3 us
    pallas_call x1, Pallas kernels: 21.6 us -> 21.1 us  [per_device(): pl.pallas_call(functools.partial(kernel, banks, segs, chunks, give), out_...]
where the time goes in v3:
time: 23.7 us; the launch traced here: 23.6 us
  Pallas kernels  22.3 us (94%)
  between operations  1.28 us (5%)
    pallas_call x1, Pallas kernels, per_device(): pl.pallas_call(functools.partial(kernel, banks, segs, chunks, give), out_...  21.1 us
    pallas_call x1, Pallas kernels, per_device(): pl.pallas_call(unpack, out_shape=[jax.ShapeDtypeStruct((1, count), jnp.fl...  1.2 us

profile of v3, /device:TPU:0, one launch (start us, length us, event | category | flops | bytes accessed | tf_op | source)
XLA Modules:
  0.0 23.6 jit_solution(12048898122537391838)
XLA Ops:
  1.3 21.1 %search.1.out_ref = f32[8,128]{1,0:T(8,128)} custom-call(bf16[4,128,128]{2,1,0:T(8,128)(2,1)} %bitcast.12, bf16[512,128]{1,0:T(8,128)(2,1)} %bitcast.13, s32[1,1]{1,0:T(1,128)} %bitcast.11.bins_ref, bf16[256,768]{1,0:T(8,128)(2,1)} %constant.8.clone.first_hbm, bf16[768,256]{1,0:T(8,128)(2,1)} %constant.9.clone.last_hbm, ...), custom_call_target="tpu_custom_call" | custom-call | tf_op jit(solution)/shard_map/search/pallas_call | solution.py:368
  22.3 1.2 %unpack.1 = (f32[1,4]{1,0:T(1,128)}, f32[4]{0:T(128)}, f32[1]{0:T(128)}) custom-call(f32[8,128]{1,0:T(8,128)} %search.1.out_ref), custom_call_target="tpu_custom_call" | custom-call | tf_op jit(solution)/shard_map/unpack/pallas_call | solution.py:408
